TPU v7x, 16 devices: a 4x2x1 block of a 4x4x8 slice. The times are simulated.
16 devices in a mesh: rep: 4 (over y, z, core), dp: 4 (over x).
Axes of the slice: x: 4, y: 2, z: 1, core: 2. Of those that a mesh axis runs over, the one named last changes fastest.
The devices are a block of a 4x4x8 slice.
Arguments:
- a: bfloat16 [16, 4, 4096, 896], P(('rep', 'dp')), parts along dimension 0
- g: bfloat16 [16, 4, 4096, 2560], P(('rep', 'dp')), parts along dimension 0
Outputs:
- output: bfloat16 [16, 896, 2560], P('rep'), parts along dimension 0
There are 4 independent parts. A program takes and returns all parts, laid end to end along the dimension named above; each array names one.
All inputs are finite; a program needn't handle non-finite values.
Results may differ from a plain program's by a relative error of at most 0.012.
Values are sent between devices in bfloat16 or wider.
A program may use at most 768 MiB of HBM per device.

v0:
```python
import jax
import jax.numpy as jnp


def solution(mesh):
    groups = mesh.shape["rep"]

    def step(a, g):
        a, g = (t.reshape(groups, -1, *t.shape[1:]) for t in (a, g))
        sums = jnp.einsum("rsntd,rsntf->rndf", a, g, preferred_element_type=jnp.float32)
        return sums.astype(jnp.bfloat16).reshape(-1, *sums.shape[2:])

    return step
```

profile of v0, /device:TPU:112, one launch (start us, length us, event | category | flops | bytes accessed | tf_op | source)
XLA Modules:
  0.0 709.4 jit_solution(15661117033576985744)
XLA Ops:
  0.0 87.3 %fusion.3 = f32[1,4,896,2560]{3,2,1,0:T(8,128)} fusion(bf16[1,4,4096,2560]{3,2,1,0:T(8,128)(2,1)} %param.1, bf16[1,4,4096,896]{3,2,1,0:T(8,128)(2,1)} %param), kind=kOutput, calls=%fused_computation.3 | convolution fusion | flops 75161927680 | bytes 149946368 | tf_op jit(solution)/rsntd,rsntf->rndf/dot_general | solution.py:10
  87.3 622.1 %all-reduce.2 = bf16[1,4,896,2560]{3,2,1,0:T(8,128)(2,1)} all-reduce(f32[1,4,896,2560]{3,2,1,0:T(8,128)} %fusion.3), channel_id=1, replica_groups=[4,4]<=[16], use_global_device_ids=true, to_apply=%add.clone | all-reduce | flops 9175040 | bytes 55050240 | tf_op jit(solution)/rsntd,rsntf->rndf/dot_general | solution.py:10
where the time goes:
time: 710 us; the launch traced here: 709 us
  blocking collectives  622 us (88%)
  matrix products  87.3 us (12%)
    dot_general x1, blocking collectives, step(): jnp.einsum('rsntd,rsntf->rndf', a, g, preferred_element_type=jnp.float32)  622 us
    dot_general x1, matrix products, step(): jnp.einsum('rsntd,rsntf->rndf', a, g, preferred_element_type=jnp.float32)  87.3 us

commit v1 on v0

v1 whole, which is shorter than its diff:
```python
import functools

import jax
import jax.numpy as jnp
from jax import lax
from jax.experimental import pallas as pl
from jax.experimental.pallas import tpu as pltpu
from jax.sharding import PartitionSpec as P

COLS = 256
HEAD = 128
ROWS = 448


def kernel(n, blocks, a_ref, g_ref, o_ref, at, gbuf, abuf, asem, gsem, ssem, rsem):
    mats, d, tokens = at.shape
    tiles = o_ref.shape[2] // COLS
    heads = d // HEAD
    slots = abuf.shape[0]
    me = lax.axis_index("dp")
    peers = (lax.rem(me + 1, n), lax.rem(me + n - 1, n))

    def unit(s, b, r):
        c = lax.rem(me + (2 * n - s if r == 0 else s), n)
        u = (b * 2 + r) * n + c
        j = lax.rem(u, tiles)
        return lax.div(u, tiles), pl.ds(pl.multiple_of(j * COLS, COLS), COLS)

    def send(s, b, r, rows=slice(None)):
        m, cols = unit(s, b, r)
        place = o_ref.at[m, rows, cols]
        return pltpu.make_async_remote_copy(
            src_ref=place,
            dst_ref=place,
            send_sem=ssem.at[s * blocks + b, r],
            recv_sem=rsem.at[s * blocks + b, r],
            device_id={"dp": peers[r]},
            device_id_type=pl.DeviceIdType.MESH,
        )

    def arrive(s, b, r):
        m, cols = unit(s + 1, b, r)
        place = o_ref.at[m, :, cols]
        pltpu.make_async_remote_copy(
            src_ref=place,
            dst_ref=place,
            send_sem=ssem.at[s * blocks + b, r],
            recv_sem=rsem.at[s * blocks + b, r],
            device_id={"dp": peers[r]},
            device_id_type=pl.DeviceIdType.MESH,
        ).wait_recv()

    def fetch_g(s, b, r, k):
        m, cols = unit(s, b, r)
        return pltpu.make_async_copy(g_ref.at[0, m, :, cols], gbuf.at[k], gsem.at[k])

    def fetch_a(q):
        m, i = lax.div(q, heads), lax.rem(q, heads)
        k = lax.rem(q, slots)
        rows = pl.ds(pl.multiple_of(i * HEAD, HEAD), HEAD)
        return pltpu.make_async_copy(a_ref.at[0, m, :, rows], abuf.at[k], asem.at[k])

    def piece(s, b, r, k, rows, add):
        m, cols = unit(s, b, r)
        total = jnp.dot(at[m, rows, :], gbuf[k], preferred_element_type=jnp.float32)
        if add:
            total += o_ref[m, rows, cols].astype(jnp.float32)
        o_ref[m, rows, cols] = total.astype(o_ref.dtype)

    barrier = pltpu.get_barrier_semaphore()
    for peer in peers:
        pl.semaphore_signal(
            barrier, inc=1, device_id={"dp": peer}, device_id_type=pl.DeviceIdType.MESH
        )
    fetch_a(0).start()
    for r in range(2):
        fetch_g(0, 0, r, r).start()
    for q in range(1, slots):
        fetch_a(q).start()
    pl.semaphore_wait(barrier, 2)

    last = mats * heads

    def first(b, _):
        k = lax.rem(b, 2) * 2
        for r in range(2):
            fetch_g(0, b + 1, r, 2 - k + r).start()
        for r in range(2):
            fetch_g(0, b, r, k + r).wait()

        def head(i, _):
            q = b * heads + i
            fetch_a(q).wait()
            rows = pl.ds(pl.multiple_of(i * HEAD, HEAD), HEAD)
            at[b, rows, :] = abuf[lax.rem(q, slots)].T

            @pl.when(q + slots < last)
            def _():
                fetch_a(q + slots).start()

            for r in range(2):
                piece(0, b, r, k + r, rows, False)
            for r in range(2):
                send(0, b, r, rows).start()
            return 0

        return lax.fori_loop(0, heads, head, 0)

    lax.fori_loop(0, mats, first, 0)

    def later(t, add, more):
        s, b = lax.div(t, blocks), lax.rem(t, blocks)
        k = lax.rem(t, 2) * 2

        def ahead():
            for r in range(2):
                s1, b1 = lax.div(t + 1, blocks), lax.rem(t + 1, blocks)
                fetch_g(s1, b1, r, 2 - k + r).start()

        if more is True:
            ahead()
        else:
            pl.when(more)(ahead)
        for r in range(2):
            fetch_g(s, b, r, k + r).wait()
            if add:
                arrive(s - 1, b, r)

            def part(i, _):
                piece(s, b, r, k + r, pl.ds(pl.multiple_of(i * ROWS, ROWS), ROWS), add)
                return 0

            lax.fori_loop(0, d // ROWS, part, 0)
            if add:
                send(s - 1, b, r).wait_send()
            send(s, b, r).start()

    for t in range(mats, blocks):
        later(jnp.int32(t), False, True)

    def reduce(t, _):
        later(t, True, t + 1 < n * blocks)
        return 0

    lax.fori_loop(blocks, n * blocks, reduce, 0)

    def gather(t, _):
        s, b = lax.div(t, blocks), lax.rem(t, blocks)
        for r in range(2):
            arrive(s - 1, b, r)
            send(s - 1, b, r).wait_send()
            send(s, b, r).start()
        return 0

    lax.fori_loop(n * blocks, (2 * n - 2) * blocks, gather, 0)

    def finish(b, _):
        for r in range(2):
            arrive(2 * n - 3, b, r)
            send(2 * n - 3, b, r).wait_send()
        return 0

    lax.fori_loop(0, blocks, finish, 0)


def solution(mesh):
    n = mesh.shape["dp"]

    def body(a, g):
        _, mats, tokens, d = a.shape
        ff = g.shape[3]
        blocks = mats * ff // COLS // (2 * n)
        return pl.pallas_call(
            functools.partial(kernel, n, blocks),
            out_shape=pltpu.VMEM((mats, d, ff), jnp.bfloat16),
            in_specs=[pl.BlockSpec(memory_space=pl.ANY)] * 2,
            out_specs=pl.BlockSpec(memory_space=pltpu.VMEM),
            scratch_shapes=[
                pltpu.VMEM((mats, d, tokens), jnp.bfloat16),
                pltpu.VMEM((4, tokens, COLS), jnp.bfloat16),
                pltpu.VMEM((3, tokens, HEAD), jnp.bfloat16),
                pltpu.SemaphoreType.DMA((3,)),
                pltpu.SemaphoreType.DMA((4,)),
                pltpu.SemaphoreType.DMA(((2 * n - 2) * blocks, 2)),
                pltpu.SemaphoreType.DMA(((2 * n - 2) * blocks, 2)),
            ],
            compiler_params=pltpu.CompilerParams(
                collective_id=0, has_side_effects=True, vmem_limit_bytes=44 * 2**20
            ),
        )(a, g)

    return jax.shard_map(
        body,
        mesh=mesh,
        in_specs=(P(("rep", "dp")), P(("rep", "dp"))),
        out_specs=P("rep"),
        check_vma=False,
    )
```

time: 710 us -> 312 us (0.44)
  blocking collectives: 622 us -> 0 us
  Pallas kernels: 0 us -> 305 us
  matrix products: 87.3 us -> 0 us
    dot_general x1 -> x0, blocking collectives: 622 us -> none  [step(): jnp.einsum('rsntd,rsntf->rndf', a, g, preferred_element_type=jnp.float32)]
    pallas_call x0 -> x1, Pallas kernels: none -> 305 us  [body(): pl.pallas_call(functools.partial(kernel, n, blocks), out_shape=pltpu.VMEM...]
    dot_general x1 -> x0, matrix products: 87.3 us -> none  [step(): jnp.einsum('rsntd,rsntf->rndf', a, g, preferred_element_type=jnp.float32)]
where the time goes in v1:
time: 312 us
  Pallas kernels  305 us (98%)
  local copies, waits for them, and re-layouts  6.68 us (2%)
    pallas_call x1, Pallas kernels, body(): pl.pallas_call(functools.partial(kernel, n, blocks), out_shape=pltpu.VMEM...  305 us
    unnamed x1, local copies, waits for them, and re-layouts  6.68 us

profile of v1, /device:TPU:112, one launch (start us, length us, event | category | flops | bytes accessed | tf_op | source)
XLA Modules:
  0.0 311.7 jit_solution(2124118478930250975)
XLA Ops:
  0.0 305.1 %shard_map.28 = bf16[4,896,2560]{2,1,0:T(8,128)(2,1)S(1)} custom-call(bf16[1,4,4096,896]{3,2,1,0:T(8,128)(2,1)} %a_ref.1, bf16[1,4,4096,2560]{3,2,1,0:T(8,128)(2,1)} %g_ref.1), custom_call_target="tpu_custom_call" | custom-call | tf_op jit(solution)/shard_map/pallas_call | solution.py:173
  305.1 6.7 %copy.4 = bf16[4,896,2560]{2,1,0:T(8,128)(2,1)} copy(bf16[4,896,2560]{2,1,0:T(8,128)(2,1)S(1)} %shard_map.28) | data formatting | bytes 36700160

commit v2 on v1

--- a/solution.py
+++ b/solution.py
@@ -10,21 +10,31 @@
 COLS = 256
 HEAD = 128
 ROWS = 448
-
-
-def kernel(n, blocks, a_ref, g_ref, o_ref, at, gbuf, abuf, asem, gsem, ssem, rsem):
+SHARES = 4
+LEFT = (4, 1)
+
+
+def left_over():
+    return LEFT[0] - (LEFT[0] - LEFT[1]) * lax.rem(lax.axis_index("rep"), 2)
+
+
+def tile(n, tiles, me, s, b, r):
+    c = lax.rem(me + 2 * n + (2 * r - 1) * s, n)
+    u = (b * 2 + r) * n + c
+    j = lax.rem(u, tiles)
+    return lax.div(u, tiles), pl.ds(pl.multiple_of(j * COLS, COLS), COLS)
+
+
+def reduce_and_gather(n, blocks, a_ref, g_ref, o_ref, at, gbuf, abuf, asem, gsem, fsem, ssem, rsem):
     mats, d, tokens = at.shape
     tiles = o_ref.shape[2] // COLS
     heads = d // HEAD
     slots = abuf.shape[0]
     me = lax.axis_index("dp")
-    peers = (lax.rem(me + 1, n), lax.rem(me + n - 1, n))
+    peers = [lax.rem(me + 1 + r * (n - 2), n) for r in range(2)]
 
     def unit(s, b, r):
-        c = lax.rem(me + (2 * n - s if r == 0 else s), n)
-        u = (b * 2 + r) * n + c
-        j = lax.rem(u, tiles)
-        return lax.div(u, tiles), pl.ds(pl.multiple_of(j * COLS, COLS), COLS)
+        return tile(n, tiles, me, s, b, r)
 
     def send(s, b, r, rows=slice(None)):
         m, cols = unit(s, b, r)
@@ -34,7 +44,7 @@
             dst_ref=place,
             send_sem=ssem.at[s * blocks + b, r],
             recv_sem=rsem.at[s * blocks + b, r],
-            device_id={"dp": peers[r]},
+            device_id={"dp": lax.rem(me + 1 + r * (n - 2), n)},
             device_id_type=pl.DeviceIdType.MESH,
         )
 
@@ -72,14 +82,67 @@
         pl.semaphore_signal(
             barrier, inc=1, device_id={"dp": peer}, device_id_type=pl.DeviceIdType.MESH
         )
-    fetch_a(0).start()
+    early = lax.rem(lax.axis_index("rep"), 2)
+    m0, cols0 = unit(0, 0, early)
+    shares = [pl.ds(i * (tokens // SHARES), tokens // SHARES) for i in range(SHARES)]
+    first_a = [
+        pltpu.make_async_copy(
+            a_ref.at[0, 0, t, pl.ds(0, HEAD)], abuf.at[0, t], fsem.at[0, i]
+        )
+        for i, t in enumerate(shares)
+    ]
+    first_g = [
+        pltpu.make_async_copy(g_ref.at[0, m0, t, cols0], gbuf.at[early, t], fsem.at[1, i])
+        for i, t in enumerate(shares)
+    ]
+    for i in range(SHARES):
+        first_a[i].start()
+        first_g[i].start()
+
+    last = mats * heads
+
+    def turn(b, i):
+        q = b * heads + i
+        fetch_a(q).wait()
+        rows = pl.ds(pl.multiple_of(i * HEAD, HEAD), HEAD)
+        at[b, rows, :] = abuf[lax.rem(q, slots)].T
+
+        @pl.when(q + slots < last)
+        def _():
+            fetch_a(q + slots).start()
+
+        return rows
+
+    def head(b, k, i):
+        rows = turn(b, i)
+        for r in range(2):
+            piece(0, b, r, k + r, rows, False)
+        for r in range(2):
+            send(0, b, r, rows).start()
+        return 0
+
+    rows = pl.ds(0, HEAD)
+    total = jnp.zeros((HEAD, COLS), jnp.float32)
+    for i, t in enumerate(shares):
+        first_a[i].wait()
+        at[0, rows, t] = abuf[0, t].T
+        first_g[i].wait()
+        if i == 0:
+            fetch_g(0, 0, 1 - early, 1 - early).start()
+        if i == SHARES - 1:
+            for q in range(1, slots):
+                fetch_a(q).start()
+        total += jnp.dot(at[0, rows, t], gbuf[early, t], preferred_element_type=jnp.float32)
+    o_ref[m0, rows, cols0] = total.astype(o_ref.dtype)
+    fetch_a(slots).start()
+    pl.semaphore_wait(barrier, 2)
+    send(0, 0, early, rows).start()
+    fetch_g(0, 0, 1 - early, 1 - early).wait()
+    piece(0, 0, 1 - early, 1 - early, rows, False)
     for r in range(2):
-        fetch_g(0, 0, r, r).start()
-    for q in range(1, slots):
-        fetch_a(q).start()
-    pl.semaphore_wait(barrier, 2)
-
-    last = mats * heads
+        fetch_g(0, 1, r, 2 + r).start()
+    send(0, 0, 1 - early, rows).start()
+    lax.fori_loop(1, heads, lambda i, _: head(jnp.int32(0), 0, i), 0)
 
     def first(b, _):
         k = lax.rem(b, 2) * 2
@@ -87,26 +150,9 @@
             fetch_g(0, b + 1, r, 2 - k + r).start()
         for r in range(2):
             fetch_g(0, b, r, k + r).wait()
-
-        def head(i, _):
-            q = b * heads + i
-            fetch_a(q).wait()
-            rows = pl.ds(pl.multiple_of(i * HEAD, HEAD), HEAD)
-            at[b, rows, :] = abuf[lax.rem(q, slots)].T
-
-            @pl.when(q + slots < last)
-            def _():
-                fetch_a(q + slots).start()
-
-            for r in range(2):
-                piece(0, b, r, k + r, rows, False)
-            for r in range(2):
-                send(0, b, r, rows).start()
-            return 0
-
-        return lax.fori_loop(0, heads, head, 0)
-
-    lax.fori_loop(0, mats, first, 0)
+        return lax.fori_loop(0, heads, lambda i, _: head(b, k, i), 0)
+
+    lax.fori_loop(1, mats, first, 0)
 
     def later(t, add, more):
         s, b = lax.div(t, blocks), lax.rem(t, blocks)
@@ -152,15 +198,88 @@
             send(s, b, r).start()
         return 0
 
-    lax.fori_loop(n * blocks, (2 * n - 2) * blocks, gather, 0)
-
-    def finish(b, _):
-        for r in range(2):
-            arrive(2 * n - 3, b, r)
-            send(2 * n - 3, b, r).wait_send()
-        return 0
-
-    lax.fori_loop(0, blocks, finish, 0)
+    end = (2 * n - 2) * blocks - left_over()
+    lax.fori_loop(n * blocks, end, gather, 0)
+
+    def finish(t, _):
+        s, b = lax.div(t, blocks), lax.rem(t, blocks)
+        for r in range(2):
+            arrive(s, b, r)
+            send(s, b, r).wait_send()
+        return 0
+
+    lax.fori_loop(end - blocks, end, finish, 0)
+
+
+def copy_out(o_ref, out_ref, sems):
+    copies = [
+        pltpu.make_async_copy(o_ref.at[m], out_ref.at[m], sems.at[m])
+        for m in range(o_ref.shape[0])
+    ]
+    for copy in copies:
+        copy.start()
+    for copy in copies:
+        copy.wait()
+
+
+def last_hops(n, blocks, o_ref, _, p_ref, ssem, rsem):
+    me = lax.axis_index("dp")
+    peers = [lax.rem(me + 1 + r * (n - 2), n) for r in range(2)]
+    barrier = pltpu.get_barrier_semaphore()
+    for peer in peers:
+        pl.semaphore_signal(
+            barrier, inc=1, device_id={"dp": peer}, device_id_type=pl.DeviceIdType.MESH
+        )
+    pl.semaphore_wait(barrier, 2)
+
+    def hop(b, r):
+        m, cols = tile(n, o_ref.shape[2] // COLS, me, 2 * n - 3, b, r)
+        return pltpu.make_async_remote_copy(
+            src_ref=o_ref.at[m, :, cols],
+            dst_ref=p_ref.at[b * 2 + r],
+            send_sem=ssem.at[b, r],
+            recv_sem=rsem.at[b, r],
+            device_id={"dp": peers[r]},
+            device_id_type=pl.DeviceIdType.MESH,
+        )
+
+    def start(b, _):
+        for r in range(2):
+            hop(b, r).start()
+        return 0
+
+    def wait(b, _):
+        for r in range(2):
+            hop(b, r).wait()
+        return 0
+
+    first = blocks - left_over()
+    lax.fori_loop(first, blocks, start, 0)
+    lax.fori_loop(first, blocks, wait, 0)
+
+
+def copy_rest(n, blocks, p_ref, _, out_ref, sems):
+    me = lax.axis_index("dp")
+
+    def put(b, r):
+        m, cols = tile(n, out_ref.shape[2] // COLS, me, 2 * n - 2, b, r)
+        return pltpu.make_async_copy(
+            p_ref.at[b * 2 + r], out_ref.at[m, :, cols], sems.at[b, r]
+        )
+
+    def start(b, _):
+        for r in range(2):
+            put(b, r).start()
+        return 0
+
+    def wait(b, _):
+        for r in range(2):
+            put(b, r).wait()
+        return 0
+
+    first = blocks - left_over()
+    lax.fori_loop(first, blocks, start, 0)
+    lax.fori_loop(first, blocks, wait, 0)
 
 
 def solution(mesh):
@@ -170,24 +289,58 @@
         _, mats, tokens, d = a.shape
         ff = g.shape[3]
         blocks = mats * ff // COLS // (2 * n)
-        return pl.pallas_call(
-            functools.partial(kernel, n, blocks),
+        hbm = pl.BlockSpec(memory_space=pltpu.HBM)
+        vmem = pl.BlockSpec(memory_space=pltpu.VMEM)
+        count = (2 * n - 2) * blocks
+        sums = pl.pallas_call(
+            functools.partial(reduce_and_gather, n, blocks),
             out_shape=pltpu.VMEM((mats, d, ff), jnp.bfloat16),
-            in_specs=[pl.BlockSpec(memory_space=pl.ANY)] * 2,
-            out_specs=pl.BlockSpec(memory_space=pltpu.VMEM),
+            in_specs=[hbm] * 2,
+            out_specs=vmem,
             scratch_shapes=[
                 pltpu.VMEM((mats, d, tokens), jnp.bfloat16),
                 pltpu.VMEM((4, tokens, COLS), jnp.bfloat16),
                 pltpu.VMEM((3, tokens, HEAD), jnp.bfloat16),
                 pltpu.SemaphoreType.DMA((3,)),
                 pltpu.SemaphoreType.DMA((4,)),
-                pltpu.SemaphoreType.DMA(((2 * n - 2) * blocks, 2)),
-                pltpu.SemaphoreType.DMA(((2 * n - 2) * blocks, 2)),
+                pltpu.SemaphoreType.DMA((2, SHARES)),
+                pltpu.SemaphoreType.DMA((count, 2)),
+                pltpu.SemaphoreType.DMA((count, 2)),
             ],
             compiler_params=pltpu.CompilerParams(
                 collective_id=0, has_side_effects=True, vmem_limit_bytes=44 * 2**20
             ),
         )(a, g)
+        sums = pltpu.with_memory_space_constraint(sums, pltpu.VMEM)
+        out = pl.pallas_call(
+            copy_out,
+            out_shape=jax.ShapeDtypeStruct((mats, d, ff), jnp.bfloat16),
+            in_specs=[vmem],
+            out_specs=hbm,
+            scratch_shapes=[pltpu.SemaphoreType.DMA((mats,))],
+            compiler_params=pltpu.CompilerParams(vmem_limit_bytes=2**20),
+        )(sums)
+        out = pltpu.with_memory_space_constraint(out, pltpu.HBM)
+        rest = pl.pallas_call(
+            functools.partial(last_hops, n, blocks),
+            out_shape=pltpu.VMEM((blocks * 2, d, COLS), jnp.bfloat16),
+            in_specs=[vmem, hbm],
+            out_specs=vmem,
+            scratch_shapes=[pltpu.SemaphoreType.DMA((blocks, 2))] * 2,
+            compiler_params=pltpu.CompilerParams(
+                collective_id=1, has_side_effects=True, vmem_limit_bytes=2**20
+            ),
+        )(sums, out)
+        rest = pltpu.with_memory_space_constraint(rest, pltpu.VMEM)
+        return pl.pallas_call(
+            functools.partial(copy_rest, n, blocks),
+            out_shape=jax.ShapeDtypeStruct((mats, d, ff), jnp.bfloat16),
+            in_specs=[vmem, hbm],
+            out_specs=hbm,
+            input_output_aliases={1: 0},
+            scratch_shapes=[pltpu.SemaphoreType.DMA((blocks, 2))],
+            compiler_params=pltpu.CompilerParams(vmem_limit_bytes=2**20),
+        )(rest, out)
 
     return jax.shard_map(
         body,

time: 312 us -> 305 us (0.978)
  local copies, waits for them, and re-layouts: 6.68 us -> 0 us
    unnamed x1 -> x0, local copies, waits for them, and re-layouts: 6.68 us -> none
    pallas_call x1 -> x4, Pallas kernels: 305 us -> 305 us  [the longest x1 265 us: body(): pl.pallas_call(functools.partial(reduce_and_gather, n, blocks), out_shape...]
where the time goes in v2:
time: 305 us
  Pallas kernels  305 us (100%)
    pallas_call x1, Pallas kernels, body(): pl.pallas_call(functools.partial(reduce_and_gather, n, blocks), out_shape...  265 us
    pallas_call x1, Pallas kernels, body(): pl.pallas_call(functools.partial(last_hops, n, blocks), out_shape=pltpu.V...  31.4 us
    pallas_call x1, Pallas kernels, body(): pl.pallas_call(copy_out, out_shape=jax.ShapeDtypeStruct((mats, d, ff), jn...  6.45 us

profile of v2, /device:TPU:112, one launch (start us, length us, event | category | flops | bytes accessed | tf_op | source)
XLA Modules:
  0.0 305.0 jit_solution(4107376181550153856)
XLA Ops:
  0.0 265.2 %shard_map.28.o_ref = bf16[4,896,2560]{2,1,0:T(8,128)(2,1)S(1)} custom-call(bf16[1,4,4096,896]{3,2,1,0:T(8,128)(2,1)} %a_ref.1, bf16[1,4,4096,2560]{3,2,1,0:T(8,128)(2,1)} %g_ref.1), custom_call_target="tpu_custom_call" | custom-call | tf_op jit(solution)/shard_map/pallas_call | solution.py:295
  265.2 6.4 %shard_map.29._ = bf16[4,896,2560]{2,1,0:T(8,128)(2,1)} custom-call(bf16[4,896,2560]{2,1,0:T(8,128)(2,1)S(1)} %shard_map.28.o_ref), custom_call_target="tpu_custom_call" | custom-call | tf_op jit(solution)/shard_map/pallas_call | solution.py:315
  271.6 31.4 %shard_map.30.p_ref = bf16[10,896,256]{2,1,0:T(8,128)(2,1)S(1)} custom-call(bf16[4,896,2560]{2,1,0:T(8,128)(2,1)S(1)} %shard_map.28.o_ref, bf16[4,896,2560]{2,1,0:T(8,128)(2,1)} %shard_map.29._), custom_call_target="tpu_custom_call" | custom-call | tf_op jit(solution)/shard_map/pallas_call | solution.py:324
  303.1 1.9 shard_map.31

commit v3 on v2

--- a/solution.py
+++ b/solution.py
@@ -11,7 +11,7 @@
 HEAD = 128
 ROWS = 448
 SHARES = 4
-LEFT = (4, 1)
+LEFT = (1, 4)
 
 
 def left_over():
@@ -19,7 +19,7 @@
 
 
 def tile(n, tiles, me, s, b, r):
-    c = lax.rem(me + 2 * n + (2 * r - 1) * s, n)
+    c = lax.rem(me + 4 * n + (2 * r - 1) * s, n)
     u = (b * 2 + r) * n + c
     j = lax.rem(u, tiles)
     return lax.div(u, tiles), pl.ds(pl.multiple_of(j * COLS, COLS), COLS)
@@ -211,15 +211,28 @@
     lax.fori_loop(end - blocks, end, finish, 0)
 
 
-def copy_out(o_ref, out_ref, sems):
-    copies = [
-        pltpu.make_async_copy(o_ref.at[m], out_ref.at[m], sems.at[m])
-        for m in range(o_ref.shape[0])
-    ]
-    for copy in copies:
-        copy.start()
-    for copy in copies:
-        copy.wait()
+def copy_out(n, blocks, o_ref, out_ref, sems):
+    me = lax.axis_index("dp")
+    first = blocks - left_over()
+
+    def put(b, r, i):
+        m, cols = tile(n, o_ref.shape[2] // COLS, me, 2 * n - 2 + i, b, r)
+        return pltpu.make_async_copy(
+            o_ref.at[m, :, cols], out_ref.at[m, :, cols], sems.at[b, r * n + i]
+        )
+
+    def each(which, act):
+        def step(b, _):
+            for r in range(2):
+                for i in which:
+                    act(put(b, r, i))
+            return 0
+
+        return step
+
+    for act in (lambda copy: copy.start(), lambda copy: copy.wait()):
+        lax.fori_loop(0, blocks, each(range(1, n), act), 0)
+        lax.fori_loop(0, first, each(range(1), act), 0)
 
 
 def last_hops(n, blocks, o_ref, _, p_ref, ssem, rsem):
@@ -313,11 +326,11 @@
         )(a, g)
         sums = pltpu.with_memory_space_constraint(sums, pltpu.VMEM)
         out = pl.pallas_call(
-            copy_out,
+            functools.partial(copy_out, n, blocks),
             out_shape=jax.ShapeDtypeStruct((mats, d, ff), jnp.bfloat16),
             in_specs=[vmem],
             out_specs=hbm,
-            scratch_shapes=[pltpu.SemaphoreType.DMA((mats,))],
+            scratch_shapes=[pltpu.SemaphoreType.DMA((blocks, 2 * n))],
             compiler_params=pltpu.CompilerParams(vmem_limit_bytes=2**20),
         )(sums)
         out = pltpu.with_memory_space_constraint(out, pltpu.HBM)

time: 305 us -> 304 us (level)
    pallas_call x1, Pallas kernels: 265 us -> 284 us  [body(): pl.pallas_call(functools.partial(reduce_and_gather, n, blocks), out_shape...]
    pallas_call x1, Pallas kernels: 31.4 us -> 12.7 us  [body(): pl.pallas_call(functools.partial(last_hops, n, blocks), out_shape=pltpu.V...]
where the time goes in v3:
time: 304 us
  Pallas kernels  304 us (100%)
    pallas_call x1, Pallas kernels, body(): pl.pallas_call(functools.partial(reduce_and_gather, n, blocks), out_shape...  284 us
    pallas_call x1, Pallas kernels, body(): pl.pallas_call(functools.partial(last_hops, n, blocks), out_shape=pltpu.V...  12.7 us
    pallas_call x1, Pallas kernels, body(): pl.pallas_call(functools.partial(copy_out, n, blocks), out_shape=jax.Shap...  6.38 us

profile of v3, /device:TPU:112, one launch (start us, length us, event | category | flops | bytes accessed | tf_op | source)
XLA Modules:
  0.0 304.1 jit_solution(16890091852289362698)
XLA Ops:
  0.0 283.9 %shard_map.28.o_ref = bf16[4,896,2560]{2,1,0:T(8,128)(2,1)S(1)} custom-call(bf16[1,4,4096,896]{3,2,1,0:T(8,128)(2,1)} %a_ref.1, bf16[1,4,4096,2560]{3,2,1,0:T(8,128)(2,1)} %g_ref.1), custom_call_target="tpu_custom_call" | custom-call | tf_op jit(solution)/shard_map/pallas_call | solution.py:308
  283.9 6.4 %shard_map.29._ = bf16[4,896,2560]{2,1,0:T(8,128)(2,1)} custom-call(bf16[4,896,2560]{2,1,0:T(8,128)(2,1)S(1)} %shard_map.28.o_ref), custom_call_target="tpu_custom_call" | custom-call | tf_op jit(solution)/shard_map/pallas_call | solution.py:328
  290.3 12.7 %shard_map.30.p_ref = bf16[10,896,256]{2,1,0:T(8,128)(2,1)S(1)} custom-call(bf16[4,896,2560]{2,1,0:T(8,128)(2,1)S(1)} %shard_map.28.o_ref, bf16[4,896,2560]{2,1,0:T(8,128)(2,1)} %shard_map.29._), custom_call_target="tpu_custom_call" | custom-call | tf_op jit(solution)/shard_map/pallas_call | solution.py:337
  303.1 1.0 shard_map.31

commit v4 on v3

--- a/solution.py
+++ b/solution.py
@@ -82,8 +82,7 @@
         pl.semaphore_signal(
             barrier, inc=1, device_id={"dp": peer}, device_id_type=pl.DeviceIdType.MESH
         )
-    early = lax.rem(lax.axis_index("rep"), 2)
-    m0, cols0 = unit(0, 0, early)
+    m0, cols0 = unit(0, 0, 0)
     shares = [pl.ds(i * (tokens // SHARES), tokens // SHARES) for i in range(SHARES)]
     first_a = [
         pltpu.make_async_copy(
@@ -92,12 +91,13 @@
         for i, t in enumerate(shares)
     ]
     first_g = [
-        pltpu.make_async_copy(g_ref.at[0, m0, t, cols0], gbuf.at[early, t], fsem.at[1, i])
+        pltpu.make_async_copy(g_ref.at[0, m0, t, cols0], gbuf.at[0, t], fsem.at[1, i])
         for i, t in enumerate(shares)
     ]
     for i in range(SHARES):
         first_a[i].start()
         first_g[i].start()
+    fetch_g(0, 0, 1, 1).start()
 
     last = mats * heads
 
@@ -127,21 +127,19 @@
         first_a[i].wait()
         at[0, rows, t] = abuf[0, t].T
         first_g[i].wait()
-        if i == 0:
-            fetch_g(0, 0, 1 - early, 1 - early).start()
         if i == SHARES - 1:
             for q in range(1, slots):
                 fetch_a(q).start()
-        total += jnp.dot(at[0, rows, t], gbuf[early, t], preferred_element_type=jnp.float32)
+        total += jnp.dot(at[0, rows, t], gbuf[0, t], preferred_element_type=jnp.float32)
     o_ref[m0, rows, cols0] = total.astype(o_ref.dtype)
     fetch_a(slots).start()
     pl.semaphore_wait(barrier, 2)
-    send(0, 0, early, rows).start()
-    fetch_g(0, 0, 1 - early, 1 - early).wait()
-    piece(0, 0, 1 - early, 1 - early, rows, False)
+    send(0, 0, 0, rows).start()
+    fetch_g(0, 0, 1, 1).wait()
+    piece(0, 0, 1, 1, rows, False)
     for r in range(2):
         fetch_g(0, 1, r, 2 + r).start()
-    send(0, 0, 1 - early, rows).start()
+    send(0, 0, 1, rows).start()
     lax.fori_loop(1, heads, lambda i, _: head(jnp.int32(0), 0, i), 0)
 
     def first(b, _):

time: 304 us -> 304 us (level)
  no operation moved by 1% of the time
where the time goes in v4:
time: 304 us
  Pallas kernels  304 us (100%)
    pallas_call x1, Pallas kernels, body(): pl.pallas_call(functools.partial(reduce_and_gather, n, blocks), out_shape...  284 us
    pallas_call x1, Pallas kernels, body(): pl.pallas_call(functools.partial(last_hops, n, blocks), out_shape=pltpu.V...  12.7 us
    pallas_call x1, Pallas kernels, body(): pl.pallas_call(functools.partial(copy_out, n, blocks), out_shape=jax.Shap...  6.38 us

profile of v4, /device:TPU:112, one launch (start us, length us, event | category | flops | bytes accessed | tf_op | source)
XLA Modules:
  0.0 304.0 jit_solution(9123090268461213332)
XLA Ops:
  0.0 283.8 %shard_map.28.o_ref = bf16[4,896,2560]{2,1,0:T(8,128)(2,1)S(1)} custom-call(bf16[1,4,4096,896]{3,2,1,0:T(8,128)(2,1)} %a_ref.1, bf16[1,4,4096,2560]{3,2,1,0:T(8,128)(2,1)} %g_ref.1), custom_call_target="tpu_custom_call" | custom-call | tf_op jit(solution)/shard_map/pallas_call | solution.py:306
  283.8 6.4 %shard_map.29._ = bf16[4,896,2560]{2,1,0:T(8,128)(2,1)} custom-call(bf16[4,896,2560]{2,1,0:T(8,128)(2,1)S(1)} %shard_map.28.o_ref), custom_call_target="tpu_custom_call" | custom-call | tf_op jit(solution)/shard_map/pallas_call | solution.py:326
  290.2 12.7 %shard_map.30.p_ref = bf16[10,896,256]{2,1,0:T(8,128)(2,1)S(1)} custom-call(bf16[4,896,2560]{2,1,0:T(8,128)(2,1)S(1)} %shard_map.28.o_ref, bf16[4,896,2560]{2,1,0:T(8,128)(2,1)} %shard_map.29._), custom_call_target="tpu_custom_call" | custom-call | tf_op jit(solution)/shard_map/pallas_call | solution.py:335
  302.9 1.0 shard_map.31
